TPU v7x, 256 devices: a whole 4x4x8 slice. The times are simulated.
256 devices in a mesh: seq: 64 (over z_hi, y, x), rep: 4 (over z_lo, core).
Axes of the slice: x: 4, y: 4, z: 8 (z_hi: 4, z_lo: 2; z = z_hi * 2 + z_lo), core: 2. Of those that a mesh axis runs over, the one named last changes fastest.
Arguments:
- queries: bfloat16 [32768, 2048], P(('rep', 'seq')), parts along dimension 0, may hold values from -6 to 6
- keys: bfloat16 [32768, 2048], P(('rep', 'seq')), parts along dimension 0, may hold values from -6 to 6
- values: bfloat16 [32768, 2048], P(('rep', 'seq')), parts along dimension 0, may hold values from -6 to 6
- short_taps: float32 [3, 3, 2048], replicated, may hold values from -3.5 to 3.5
- decay: float32 [2048, 16], replicated, may hold values from 6.1035156e-05 to 0.1
- residue: float32 [2048, 16], replicated, may hold values from -1.5 to 1.5
- skip: float32 [2048], replicated, may hold values from -3 to 3
- w_out: bfloat16 [2048, 2048], replicated, may hold values from -0.125 to 0.125
Outputs:
- layer_out: bfloat16 [32768, 2048], P(('rep', 'seq')), parts along dimension 0
There are 4 independent parts, one for each index of `rep`. A program takes and returns all parts, laid end to end along the dimension named above; an argument that names none is the same for every part. Nothing has to cross between parts.
All inputs are finite; a program needn't handle non-finite values.
Results may differ from a plain program's by a relative error of at most 0.014.
Values may be sent and summed in bfloat16 or wider, within the bound.
A program may use at most 64 MiB of HBM per device.

v0:
```python
import math

import jax
import jax.numpy as jnp
from jax import lax
from jax.sharding import PartitionSpec as P


def passed_along(value, axis, by):
    devices = lax.axis_size(axis)
    pairs = [(i, i + by) for i in range(devices) if 0 <= i + by < devices]
    return lax.ppermute(value, axis, pairs)


def short_conv(tokens, before, taps):
    extended = jnp.concatenate([before, tokens], axis=0).astype(jnp.float32)
    result = taps[0] * extended[2:] + taps[1] * extended[1:-1]
    return result + taps[2] * extended[:-2]


def modal_local(sig_t, rates, weights):
    chans, length = sig_t.shape
    blk_rows = math.gcd(length, 128)
    blk_count = length // blk_rows
    group = math.gcd(chans, 128)
    groups = chans // group
    modes = rates.shape[1]
    places = jnp.arange(blk_rows, dtype=jnp.float32)
    row_idx = jnp.arange(blk_rows, dtype=jnp.int32)
    lower = row_idx[:, None] >= row_idx[None, :]

    def within(items):
        piece, grp_rates, grp_weights = items
        falling = jnp.exp(-places[None, None, :] * grp_rates[:, :, None])
        rising = jnp.exp(places[None, None, :] * grp_rates[:, :, None]) * grp_weights[:, :, None]
        toeplitz = jnp.einsum("gmi,gmj->gij", falling, rising)
        toeplitz = jnp.where(lower[None], toeplitz, 0.0)
        inner = jnp.einsum("gij,gbj->gbi", toeplitz, piece)
        end_table = jnp.exp(-(blk_rows - 1.0 - places)[None, None, :] * grp_rates[:, :, None])
        ending = jnp.einsum("gmj,gbj->gmb", end_table, piece)
        return (inner, ending)

    grouped = sig_t.reshape(groups, group, blk_count, blk_rows)
    rate_groups = rates.reshape(groups, group, modes)
    weight_groups = weights.reshape(groups, group, modes)
    inner, ending = lax.map(within, (grouped, rate_groups, weight_groups))
    inner = inner.reshape(chans, blk_count, blk_rows)
    ending = ending.reshape(chans, modes, blk_count)
    blk_idx = jnp.arange(blk_count, dtype=jnp.int32)
    gaps = (blk_idx[:, None] - blk_idx[None, :]).astype(jnp.float32)
    earlier_mask = gaps >= 0.0
    clamped = jnp.maximum(gaps, 0.0)

    def carry_mode(items):
        rate_col, end_rows = items
        linking = jnp.exp(-blk_rows * rate_col[:, None, None] * clamped[None])
        linking = jnp.where(earlier_mask[None], linking, 0.0)
        return jnp.einsum("cij,cj->ci", linking, end_rows)

    reached = lax.map(carry_mode, (rates.T, ending.transpose(1, 0, 2)))
    reached = reached.transpose(1, 0, 2)
    return (inner, reached)


def modal_finish(inner, reached, start_state, rates, weights):
    chans, blk_count, blk_rows = inner.shape
    places = jnp.arange(blk_rows, dtype=jnp.float32)
    blk_places = jnp.arange(blk_count, dtype=jnp.float32)
    entering = jnp.concatenate(
        [jnp.zeros((chans, reached.shape[1], 1), jnp.float32), reached[:, :, :-1]], axis=2
    )
    entering = (
        entering
        + jnp.exp(-blk_rows * blk_places[None, None, :] * rates[:, :, None])
        * start_state[:, :, None]
    )
    carry_table = jnp.exp(-(places + 1.0)[None, None, :] * rates[:, :, None]) * weights[:, :, None]
    carried = jnp.einsum("cmi,cmb->cbi", carry_table, entering)
    return (inner + carried).reshape(chans, blk_count * blk_rows)


def body(queries, keys, values, short_taps, decay, residue, skip, w_out):
    tok_rows = queries.shape[0]
    tails = jnp.stack([queries[tok_rows - 2 :], keys[tok_rows - 2 :], values[tok_rows - 2 :]])
    before = passed_along(tails, "seq", 1)
    q_short = short_conv(queries, before[0], short_taps[0])
    k_short = short_conv(keys, before[1], short_taps[1])
    v_short = short_conv(values, before[2], short_taps[2])
    mixed_in = (k_short * v_short).astype(jnp.bfloat16)
    weights = residue * jnp.sqrt(1.0 - jnp.exp(-2.0 * decay))
    mixed_t = mixed_in.T
    chans = decay.shape[0] // lax.axis_size("seq")
    spread = lax.all_to_all(mixed_t, "seq", split_axis=0, concat_axis=1, tiled=True)
    first_chan = lax.axis_index("seq") * chans
    rates_mine = lax.dynamic_slice_in_dim(decay, first_chan, chans, 0)
    weights_mine = lax.dynamic_slice_in_dim(weights, first_chan, chans, 0)
    skip_mine = lax.dynamic_slice_in_dim(skip, first_chan, chans, 0)
    signal = spread.astype(jnp.float32)
    inner, reached = modal_local(signal, rates_mine, weights_mine)
    convolved = modal_finish(inner, reached, jnp.zeros_like(rates_mine), rates_mine, weights_mine)
    long_part = (convolved + skip_mine[:, None] * signal).astype(jnp.bfloat16)
    long_t = lax.all_to_all(long_part, "seq", split_axis=1, concat_axis=0, tiled=True)
    long_out = long_t.T
    gated = (q_short * long_out.astype(jnp.float32)).astype(jnp.bfloat16)
    return jnp.dot(gated, w_out, preferred_element_type=jnp.float32).astype(jnp.bfloat16)


def solution(mesh):
    placed = (
        P(("rep", "seq"), None),
        P(("rep", "seq"), None),
        P(("rep", "seq"), None),
        P(),
        P(),
        P(),
        P(),
        P(),
    )
    return jax.shard_map(
        body, mesh=mesh, in_specs=placed, out_specs=P(("rep", "seq"), None), check_vma=False
    )
```

profile of v0, /device:TPU:1, one launch (start us, length us, event | category | flops | bytes accessed | tf_op | source)
XLA Modules:
  0.0 91.8 jit_solution(10317764866472194176)
XLA Ops:
  0.0 0.8 slice_bitcast_fusion.2
  0.8 0.8 slice_bitcast_fusion
  1.6 3.9 %collective-permute-start = (bf16[3,2,2048]{2,1,0:T(2,128)(2,1)S(1)}, bf16[3,2,2048]{2,1,0:T(2,128)(2,1)S(1)}, u32[]{:S(2)}, u32[]{:S(2)}) collective-permute-start(bf16[3,2,2048]{2,1,0:T(2,128)(2,1)S(1)} %pad_maximum_fusion), channel_id=1, source_target_pairs={{0,4},{4,8},{8,12},{12,16},{16,20},{20,24},{24,28},{28,32},{32,36}... | collective-permute-start | bytes 73736 | tf_op jit(solution)/shard_map/ppermute | solution.py:12
  5.6 1.1 %fusion.78 = (f32[1,1,2048]{2,1,0:T(1,128)S(1)}, f32[1,1,2048]{2,1,0:T(1,128)S(1)}, f32[1,1,2048]{2,1,0:T(1,128)S(1)}, f32[1,1,2048]{2,1,0:T(1,128)S(1)}, f32[1,...) fusion(f32[3,3,2048]{2,1,0:T(4,128)} %param.13), kind=kLoop, calls=%fused_computation.91 | loop fusion | bytes 147456 | tf_op jit(solution)/shard_map/slice | solution.py:17
  6.6 1.3 %copy.26 = bf16[128,2048]{0,1:T(8,128)(2,1)S(1)} copy(bf16[128,2048]{1,0:T(8,128)(2,1)} %param.11) | data formatting | bytes 1048576 | tf_op args[1]
  7.9 1.3 %copy.28 = bf16[128,2048]{0,1:T(8,128)(2,1)S(1)} copy(bf16[128,2048]{1,0:T(8,128)(2,1)} %param.12) | data formatting | bytes 1048576 | tf_op args[2]
  9.3 0.0 collective-permute-done
  9.3 0.3 copy.39
  9.6 0.3 copy.40
  9.9 0.4 maximum_convert_fusion.1
  10.4 0.4 maximum_convert_fusion.2
  10.8 3.7 %fusion.33 = bf16[128,2048]{0,1:T(8,128)(2,1)} fusion(f32[130,2048]{0,1:T(8,128)S(1)} %maximum_convert_fusion.2, f32[130,2048]{0,1:T(8,128)S(1)} %maximum_convert_fusion.1, f32[2048]{0:T(1024)S(1)} %bitcast.74, f32[2048]{0:T(1024)S(1)} %bitcast.75, f32[2048]{0:T(1024)S(1)} %bitcast.71, f32[2048]{0:T(1024)S(1)} %bitcast.72, f32[2048]{0:T(1024)S(1)} %bitcast.73, ...), kind=kLoop, calls=%fused_computation.32 | loop fusion | flops 3145728 | bytes 6864896 | tf_op jit(solution)/shard_map/convert_element_type | solution.py:89
  14.5 14.0 %all-to-all-start = ((bf16[64,32,128]{2,1,0:T(8,128)(2,1)}), bf16[64,32,128]{2,1,0:T(8,128)(2,1)S(1)}, u32[]{:S(2)}, u32[]{:S(2)}) async-start(bf16[64,32,128]{2,1,0:T(8,128)(2,1)} %bitcast.16), calls=%async_computation | async-start | bytes 1048576 | tf_op jit(solution)/shard_map/all_to_all | solution.py:93
  28.5 0.8 dynamic-slice_multiply_fusion
  29.3 0.1 copy.30
  29.4 0.1 copy.31
  29.5 0.8 dynamic_slice.27
  30.3 14.8 %all-to-all-done = bf16[64,32,128]{2,1,0:T(8,128)(2,1)S(1)} async-done(((bf16[64,32,128]{2,1,0:T(8,128)(2,1)}), bf16[64,32,128]{2,1,0:T(8,128)(2,1)S(1)}, u32[]{:S(2)}, u32[]{:S(2)}) %all-to-all-start) | async-done | bytes 524320 | tf_op jit(solution)/shard_map/all_to_all | solution.py:93
  45.1 0.4 convolution_bitcast_fusion
  45.5 8.3 %while.3 = (s32[]{:T(128)}, f32[16,32,64]{2,1,0:T(8,128)S(1)}, f32[16,32]{1,0:T(8,128)S(1)}, bf16[16,32,64]{2,0,1:T(8,128)(2,1)S(1)}, s32[]{:T(128)}) while((s32[]{:T(128)}, f32[16,32,64]{2,1,0:T(8,128)S(1)}, f32[16,32]{1,0:T(8,128)S(1)}, bf16[16,32,64]{2,0,1:T(8,128)(2,1)S(1)}, s32[]{:T(128)}) %tuple.39), condition=%wide.region_1.2_spmd.clone, body=%wide.region_0.1_spmd.clone.sunk | while | flops 548898 | bytes 119625 | solution.py:60
  45.6 0.4 fusion.89
  46.1 0.4 fusion.89
  46.6 0.4 fusion.89
  47.1 0.4 fusion.89
  47.6 0.4 fusion.89
  48.2 0.4 fusion.89
  48.7 0.4 fusion.89
  49.2 0.4 fusion.89
  49.7 0.4 fusion.89
  50.2 0.4 fusion.89
  50.7 0.4 fusion.89
  51.3 0.4 fusion.89
  51.8 0.4 fusion.89
  52.3 0.4 fusion.89
  52.8 0.4 fusion.89
  53.3 0.4 fusion.89
  53.8 0.2 multiply_add_fusion
  54.0 0.5 fusion.47
  54.5 0.0 copy-start
  54.5 1.4 %fusion.28 = bf16[32,64,128]{2,1,0:T(8,128)(2,1)S(1)} fusion(f32[32,64,128]{2,1,0:T(8,128)S(1)} %fusion.47, pred[128,128]{1,0:T(8,128)(4,1)S(1)} %iota_compare_fusion, f32[32]{0:T(128)S(1)} %dynamic_slice.27, bf16[64,32,128]{2,1,0:T(8,128)(2,1)S(1)} %all-to-all-done, f32[32,16]{1,0:T(8,128)S(1)} %copy.31, f32[32,16]{1,0:T(8,128)S(1)} %copy.30, ...), kind=kOutput, calls=%fused_computation.27 | convolution fusion | flops 85917696 | bytes 2118272 | tf_op jit(solution)/shard_map/while/body/eval_jaxpr/gij,gbj->gbi/dot_general | solution.py:38
  56.0 1.1 %copy.34 = bf16[32,64,128]{2,0,1:T(8,128)(2,1)} copy(bf16[32,64,128]{2,1,0:T(8,128)(2,1)S(1)} %fusion.28) | data formatting | bytes 1048576 | tf_op jit(solution)/shard_map/convert_element_type | solution.py:101
  57.1 8.5 %all-to-all-start.1 = ((bf16[32,64,128]{2,0,1:T(8,128)(2,1)}), bf16[32,64,128]{2,0,1:T(8,128)(2,1)}, u32[]{:S(2)}, u32[]{:S(2)}) async-start(bf16[32,64,128]{2,0,1:T(8,128)(2,1)} %copy.34), calls=%async_computation.1 | async-start | bytes 1048576 | tf_op jit(solution)/shard_map/all_to_all | solution.py:102
  65.6 0.0 copy-done
  65.6 0.3 copy.24
  65.9 0.3 copy.38
  66.2 0.4 maximum_convert_fusion
  66.6 17.2 %all-to-all-done.1 = bf16[32,64,128]{2,0,1:T(8,128)(2,1)} async-done(((bf16[32,64,128]{2,0,1:T(8,128)(2,1)}), bf16[32,64,128]{2,0,1:T(8,128)(2,1)}, u32[]{:S(2)}, u32[]{:S(2)}) %all-to-all-start.1) | async-done | bytes 524320 | tf_op jit(solution)/shard_map/all_to_all | solution.py:102
  83.8 2.5 %fusion.39 = bf16[128,2048]{0,1:T(8,128)(2,1)S(1)} fusion(f32[130,2048]{0,1:T(8,128)S(1)} %maximum_convert_fusion, f32[2048]{0:T(1024)S(1)} %bitcast.67, f32[2048]{0:T(1024)S(1)} %bitcast.68, f32[2048]{0:T(1024)S(1)} %bitcast.69, bf16[32,64,128]{2,0,1:T(8,128)(2,1)} %all-to-all-done.1), kind=kLoop, calls=%fused_computation.44 | loop fusion | flops 2097152 | bytes 4218880 | tf_op jit(solution)/shard_map/convert_element_type | solution.py:104
  86.3 5.5 %convolution_convert_fusion = bf16[128,2048]{1,0:T(8,128)(2,1)} fusion(bf16[128,2048]{0,1:T(8,128)(2,1)S(1)} %fusion.39, bf16[2048,2048]{1,0:T(8,128)(2,1)} %param.17), kind=kOutput, calls=%fused_computation.21 | convolution fusion | flops 1074003968 | bytes 9437184 | tf_op jit(solution)/shard_map/dot_general | solution.py:105
  (72 shorter events, 0.8 us)
Async XLA Ops:
  1.6 7.6 %collective-permute-start = (bf16[3,2,2048]{2,1,0:T(2,128)(2,1)S(1)}, bf16[3,2,2048]{2,1,0:T(2,128)(2,1)S(1)}, u32[]{:S(2)}, u32[]{:S(2)}) collective-permute-start(bf16[3,2,2048]{2,1,0:T(2,128)(2,1)S(1)} %pad_maximum_fusion), channel_id=1, source_target_pairs={{0,4},{4,8},{8,12},{12,16},{16,20},{20,24},{24,28},{28,32},{32,36}... | collective-permute-start | bytes 73736 | tf_op jit(solution)/shard_map/ppermute | solution.py:12
  14.5 30.6 %all-to-all-start = ((bf16[64,32,128]{2,1,0:T(8,128)(2,1)}), bf16[64,32,128]{2,1,0:T(8,128)(2,1)S(1)}, u32[]{:S(2)}, u32[]{:S(2)}) async-start(bf16[64,32,128]{2,1,0:T(8,128)(2,1)} %bitcast.16), calls=%async_computation | async-start | bytes 1048576 | tf_op jit(solution)/shard_map/all_to_all | solution.py:93
  54.5 11.1 %copy-start = (bf16[128,2048]{1,0:T(8,128)(2,1)S(1)}, bf16[128,2048]{1,0:T(8,128)(2,1)}, u32[]{:S(2)}) copy-start(bf16[128,2048]{1,0:T(8,128)(2,1)} %param.10) | copy-start | bytes 1572868
  57.1 26.7 %all-to-all-start.1 = ((bf16[32,64,128]{2,0,1:T(8,128)(2,1)}), bf16[32,64,128]{2,0,1:T(8,128)(2,1)}, u32[]{:S(2)}, u32[]{:S(2)}) async-start(bf16[32,64,128]{2,0,1:T(8,128)(2,1)} %copy.34), calls=%async_computation.1 | async-start | bytes 1048576 | tf_op jit(solution)/shard_map/all_to_all | solution.py:102
where the time goes:
time: 92.5 us; the launch traced here: 91.8 us
  waiting for transfers between devices  32 us (35%)
  starting transfers between devices  26.4 us (29%)
  matrix products  15 us (16%)
  other arithmetic  9.15 us (10%)
  local copies, waits for them, and re-layouts  8.63 us (9%)
    all_to_all x1, waiting for transfers between devices, body(): lax.all_to_all(long_part, 'seq', split_axis=1, concat_axis=0, tiled=True)  17.2 us
    all_to_all x1, waiting for transfers between devices, body(): lax.all_to_all(mixed_t, 'seq', split_axis=0, concat_axis=1, tiled=True)  14.8 us
    all_to_all x1, starting transfers between devices, body(): lax.all_to_all(mixed_t, 'seq', split_axis=0, concat_axis=1, tiled=True)  14 us
    all_to_all x1, starting transfers between devices, body(): lax.all_to_all(long_part, 'seq', split_axis=1, concat_axis=0, tiled=True)  8.5 us
    dot_general x16, matrix products, carry_mode(): return jnp.einsum('cij,cj->ci', linking, end_rows)  7.19 us
    dot_general x1, matrix products, body(): jnp.dot(gated, w_out, preferred_element_type=jnp.float32)  5.47 us
    ppermute x1, starting transfers between devices, passed_along(): return lax.ppermute(value, axis, pairs)  3.93 us
    unnamed x8, local copies, waits for them, and re-layouts  3.85 us
  transfers between devices with their start and end apart: 3, of which 2 were waited for; matrix products, arithmetic and copies ran while one was open for 7% of the time, Pallas kernels for 0%

commit v1 on v0

v1 whole, which is shorter than its diff:
```python
import functools

import jax
import jax.numpy as jnp
from jax import lax
from jax.experimental import pallas as pl
from jax.experimental.pallas import tpu as pltpu
from jax.sharding import PartitionSpec as P

MESH = pl.DeviceIdType.MESH
LANES = 128
ROWS = 8


def lanes(strip, count=1):
    return pl.ds(pl.multiple_of(strip * LANES, LANES), count * LANES)


def kernel(
    planes, q_hbm, k_hbm, v_hbm, taps_hbm, rate_hbm, res_hbm, skip_hbm, w_hbm, out_ref,
    q_in, k_in, v_in, tails, halos, taps, rate, res, skip, w_in,
    qf, kf, vf, x, y, gain, ends, got, sums, carry, sums_in, starts, starts_in, held, spread, gated,
    load_sem, halo_send, halo_recv, up_send, up_recv, side_send, side_recv, down_send, down_recv,
):
    toks, width = q_hbm.shape
    modes = rate_hbm.shape[0]
    strips = width // LANES
    blocks = toks // ROWS
    members = strips
    wide = min(4, strips)
    me = lax.axis_index("seq")
    plane, spot = me // members, me % members
    last = planes * members - 1

    def load(source, target, at):
        copy = pltpu.make_async_copy(source, target, load_sem.at[at])
        copy.start()
        return copy

    end_rows = pl.ds(toks - ROWS, ROWS)
    tail_loads = [load(ref.at[end_rows, :], tails.at[i], i) for i, ref in enumerate((k_hbm, v_hbm, q_hbm))]
    k_load = load(k_hbm, k_in, 3)
    v_load = load(v_hbm, v_in, 4)
    rate_load = load(rate_hbm, rate, 5)
    taps_load = load(taps_hbm, taps, 6)
    res_load = load(res_hbm, res, 7)
    skip_load = load(skip_hbm, skip, 8)
    q_load = load(q_hbm, q_in, 9)
    w_load = load(w_hbm, w_in, 10)

    barrier = pltpu.get_barrier_semaphore()

    def greet(device):
        pl.semaphore_signal(barrier, inc=1, device_id={"seq": device}, device_id_type=MESH)

    for i in range(members):

        @pl.when(spot != i)
        def _():
            greet(plane * members + i)

    for i in range(planes):

        @pl.when(plane != i)
        def _():
            greet(i * members + spot)

    first_of_plane = (spot == 0) & (plane > 0)
    last_of_plane = (spot == members - 1) & (plane < planes - 1)

    @pl.when(first_of_plane)
    def _():
        greet(me - 1)

    @pl.when(last_of_plane)
    def _():
        greet(me + 1)

    for copy in (k_load, v_load, rate_load, taps_load):
        copy.wait()

    def short(source, kind, start, count, cols):
        rows = [source[pl.ds(ROWS + start - lag, count), cols] for lag in range(3)]
        total = taps[kind, 0:1, cols] * rows[0] + taps[kind, 1:2, cols] * rows[1]
        return total + taps[kind, 2:3, cols] * rows[2]

    def mixed(start, count, cols):
        product = short(kf, 1, start, count, cols) * short(vf, 2, start, count, cols)
        x[pl.ds(start, count), cols] = product.astype(jnp.bfloat16).astype(jnp.float32)

    def first_pass(at, _):
        cols = lanes(at * wide, wide)
        kf[0:ROWS, cols] = jnp.zeros((ROWS, wide * LANES), jnp.float32)
        vf[0:ROWS, cols] = jnp.zeros((ROWS, wide * LANES), jnp.float32)
        kf[pl.ds(ROWS, toks), cols] = k_in[:, cols].astype(jnp.float32)
        vf[pl.ds(ROWS, toks), cols] = v_in[:, cols].astype(jnp.float32)
        for block in range(blocks):
            mixed(block * ROWS, ROWS, cols)
        step = jnp.exp(-rate[:, cols])
        state = jnp.zeros((modes, wide * LANES), jnp.float32)
        for t in range(2, toks):
            state = step * state + x[pl.ds(t, 1), cols]
        for i in range(wide):
            ends[at * wide + i] = state[:, i * LANES : (i + 1) * LANES]
        return 0

    lax.fori_loop(0, strips // wide, first_pass, 0)

    around = (members - 1) + (planes - 1)
    pl.semaphore_wait(barrier, around + jnp.where(first_of_plane | last_of_plane, 1, 0))

    for copy in tail_loads:
        copy.wait()

    def halo_copy(device):
        return pltpu.make_async_remote_copy(
            src_ref=tails, dst_ref=halos, send_sem=halo_send, recv_sem=halo_recv,
            device_id={"seq": device}, device_id_type=MESH,
        )

    @pl.when(me < last)
    def _():
        halo_copy(me + 1).start()

    @pl.when(me == 0)
    def _():
        for i in range(3):
            halos[i] = jnp.zeros((ROWS, width), jnp.bfloat16)

    @pl.when(me > 0)
    def _():
        halo_copy(me - 1).wait_recv()

    def patch(strip, _):
        cols = lanes(strip)
        kf[0:ROWS, cols] = halos[0, :, cols].astype(jnp.float32)
        vf[0:ROWS, cols] = halos[1, :, cols].astype(jnp.float32)
        mixed(0, ROWS, cols)
        fade = rate[:, cols]
        first = jnp.exp(-(toks - 1.0) * fade) * x[0:1, cols]
        second = jnp.exp(-(toks - 2.0) * fade) * x[1:2, cols]
        ends[strip] = ends[strip] + first + second
        return 0

    lax.fori_loop(0, strips, patch, 0)

    def up(i):
        return pltpu.make_async_remote_copy(
            src_ref=ends.at[i], dst_ref=got.at[spot], send_sem=up_send.at[i], recv_sem=up_recv.at[spot],
            device_id={"seq": plane * members + i}, device_id_type=MESH,
        )

    for i in range(members):

        @pl.when(spot != i)
        def _():
            up(i).start()

    got[spot] = ends[spot]

    for copy in (res_load, skip_load, q_load):
        copy.wait()

    places = lax.broadcasted_iota(jnp.int32, (ROWS, LANES), 0)

    def second_pass(at, _):
        cols = lanes(at * wide, wide)
        step = jnp.exp(-rate[:, cols])
        state = jnp.zeros((modes, wide * LANES), jnp.float32)
        for t in range(toks):
            if t % ROWS == 0:
                for i in range(wide):
                    held[i, t // ROWS] = state[:, i * LANES : (i + 1) * LANES]
            state = step * state + x[pl.ds(t, 1), cols]
        scale = res[:, cols] * jnp.sqrt(1.0 - jnp.exp(-2.0 * rate[:, cols]))
        qf[pl.ds(0, ROWS), cols] = halos[2, :, cols].astype(jnp.float32)
        qf[pl.ds(ROWS, toks), cols] = q_in[:, cols].astype(jnp.float32)
        for i in range(wide):
            strip = at * wide + i
            mine = lanes(strip)
            later = (places + 1).astype(jnp.float32)
            after = jnp.zeros((ROWS, LANES), jnp.float32)
            for m in range(modes):
                weight = scale[m : m + 1, i * LANES : (i + 1) * LANES]
                table = jnp.exp(-later * rate[pl.ds(m, 1), mine]) * weight
                gain[strip, m] = table
                after = after + table
            now = jnp.sum(scale[:, i * LANES : (i + 1) * LANES], axis=0, keepdims=True)
            now = now + skip[pl.ds(strip, 1), :]
            taper = jnp.where(places == 0, now, pltpu.roll(after, 1, 0))
            near = [taper] + [jnp.where(places >= j, pltpu.roll(taper, j, 0), 0.0) for j in range(1, ROWS)]
            for block in range(blocks):
                total = near[0] * x[pl.ds(block * ROWS, 1), mine]
                for j in range(1, ROWS):
                    total = total + near[j] * x[pl.ds(block * ROWS + j, 1), mine]
                if block > 0:
                    for m in range(modes):
                        total = total + gain[strip, m] * held[i, block, pl.ds(m, 1), :]
                y[pl.ds(block * ROWS, ROWS), mine] = total
        return 0

    lax.fori_loop(0, strips // wide, second_pass, 0)

    for i in range(members):

        @pl.when(spot != i)
        def _():
            pltpu.make_async_remote_copy(
                src_ref=got.at[i], dst_ref=got.at[i], send_sem=up_send.at[i], recv_sem=up_recv.at[i],
                device_id={"seq": me}, device_id_type=MESH,
            ).wait_recv()

    fade = rate[:, lanes(spot)]
    long_step = jnp.exp(-float(toks) * fade)
    total = jnp.zeros((modes, LANES), jnp.float32)
    for i in range(members):
        starts[i] = total
        total = long_step * total + got[i]
    sums[...] = total

    def side(i):
        return pltpu.make_async_remote_copy(
            src_ref=sums, dst_ref=sums_in.at[plane], send_sem=side_send.at[i], recv_sem=side_recv.at[plane],
            device_id={"seq": i * members + spot}, device_id_type=MESH,
        )

    for i in range(1, planes):

        @pl.when(plane < i)
        def _():
            side(i).start()

    def widen(strip, _):
        fade = rate[:, lanes(strip)]
        factor = jnp.exp(-float(ROWS) * fade)
        power = jnp.ones_like(factor)
        for block in range(blocks):
            spread[strip, block] = power
            power = power * factor
        return 0

    lax.fori_loop(0, strips, widen, 0)

    carry[...] = jnp.zeros((modes, LANES), jnp.float32)
    plane_step = jnp.exp(-float(toks * members) * fade)
    for i in range(planes - 1):

        @pl.when(plane > i)
        def _():
            pltpu.make_async_remote_copy(
                src_ref=sums_in.at[i], dst_ref=sums_in.at[i], send_sem=side_send.at[i], recv_sem=side_recv.at[i],
                device_id={"seq": me}, device_id_type=MESH,
            ).wait_recv()
            carry[...] = plane_step * carry[...] + sums_in[i]

    entering = carry[...]
    for i in range(members):
        starts[i] = starts[i] + jnp.exp(-float(toks * i) * fade) * entering

    def down(i):
        return pltpu.make_async_remote_copy(
            src_ref=starts.at[i], dst_ref=starts_in.at[spot], send_sem=down_send.at[i], recv_sem=down_recv.at[spot],
            device_id={"seq": plane * members + i}, device_id_type=MESH,
        )

    for i in range(members):

        @pl.when(spot != i)
        def _():
            down(i).start()

    starts_in[spot] = starts[spot]

    for i in range(members):

        @pl.when(spot != i)
        def _():
            pltpu.make_async_remote_copy(
                src_ref=starts_in.at[i], dst_ref=starts_in.at[i], send_sem=down_send.at[i], recv_sem=down_recv.at[i],
                device_id={"seq": me}, device_id_type=MESH,
            ).wait_recv()

    def last_pass(strip, _):
        cols = lanes(strip)
        entry = starts_in[strip]
        for block in range(blocks):
            held[0, block] = spread[strip, block] * entry
        for block in range(blocks):
            rows = pl.ds(block * ROWS, ROWS)
            total = y[rows, cols]
            for m in range(modes):
                total = total + gain[strip, m] * held[0, block, pl.ds(m, 1), :]
            q_short = short(qf, 0, block * ROWS, ROWS, cols)
            y[rows, cols] = q_short * total.astype(jnp.bfloat16).astype(jnp.float32)
        gated[:, cols] = y[:, cols].astype(jnp.bfloat16)
        return 0

    lax.fori_loop(0, strips, last_pass, 0)

    w_load.wait()
    column = min(256, width)

    def project(at, _):
        cols = pl.ds(pl.multiple_of(at * column, column), column)
        out_ref[:, cols] = jnp.dot(
            gated[...], w_in[:, cols], preferred_element_type=jnp.float32
        ).astype(out_ref.dtype)
        return 0

    lax.fori_loop(0, width // column, project, 0)

    @pl.when(me < last)
    def _():
        halo_copy(me + 1).wait_send()

    for i in range(members):

        @pl.when(spot != i)
        def _():
            up(i).wait_send()
            down(i).wait_send()

    for i in range(1, planes):

        @pl.when(plane < i)
        def _():
            side(i).wait_send()


def body(planes, queries, keys, values, short_taps, decay, residue, skip, w_out):
    toks, width = queries.shape
    modes = decay.shape[1]
    strips = width // LANES
    blocks = toks // ROWS
    wide = min(4, strips)
    f32, bf16 = jnp.float32, jnp.bfloat16
    dma = pltpu.SemaphoreType.DMA
    anywhere = pl.BlockSpec(memory_space=pl.ANY)
    return pl.pallas_call(
        functools.partial(kernel, planes),
        out_shape=jax.ShapeDtypeStruct((toks, width), bf16),
        in_specs=[anywhere] * 8,
        out_specs=pl.BlockSpec(memory_space=pltpu.VMEM),
        scratch_shapes=[
            pltpu.VMEM((toks, width), bf16),
            pltpu.VMEM((toks, width), bf16),
            pltpu.VMEM((toks, width), bf16),
            pltpu.VMEM((3, ROWS, width), bf16),
            pltpu.VMEM((3, ROWS, width), bf16),
            pltpu.VMEM((3, 3, width), f32),
            pltpu.VMEM((modes, width), f32),
            pltpu.VMEM((modes, width), f32),
            pltpu.VMEM((strips, LANES), f32),
            pltpu.VMEM((width, width), bf16),
            pltpu.VMEM((toks + ROWS, width), f32),
            pltpu.VMEM((toks + ROWS, width), f32),
            pltpu.VMEM((toks + ROWS, width), f32),
            pltpu.VMEM((toks, width), f32),
            pltpu.VMEM((toks, width), f32),
            pltpu.VMEM((strips, modes, ROWS, LANES), f32),
            pltpu.VMEM((strips, modes, LANES), f32),
            pltpu.VMEM((strips, modes, LANES), f32),
            pltpu.VMEM((modes, LANES), f32),
            pltpu.VMEM((modes, LANES), f32),
            pltpu.VMEM((planes, modes, LANES), f32),
            pltpu.VMEM((strips, modes, LANES), f32),
            pltpu.VMEM((strips, modes, LANES), f32),
            pltpu.VMEM((wide, blocks, modes, LANES), f32),
            pltpu.VMEM((strips, blocks, modes, LANES), f32),
            pltpu.VMEM((toks, width), bf16),
            dma((11,)),
            dma,
            dma,
            dma((strips,)),
            dma((strips,)),
            dma((planes,)),
            dma((planes,)),
            dma((strips,)),
            dma((strips,)),
        ],
        compiler_params=pltpu.CompilerParams(
            collective_id=0, has_side_effects=True, vmem_limit_bytes=60 * 1024 * 1024
        ),
    )(
        queries, keys, values, short_taps, decay.T, residue.T,
        skip.reshape(strips, LANES), w_out,
    )


def solution(mesh):
    split = P(("rep", "seq"), None)
    placed = (split, split, split, P(), P(), P(), P(), P())

    def run(queries, *rest):
        planes = mesh.shape["seq"] * LANES // queries.shape[1]
        return body(planes, queries, *rest)

    return jax.shard_map(run, mesh=mesh, in_specs=placed, out_specs=split, check_vma=False)
```

time: 92.5 us -> 37.8 us (0.41)
  the two profiles are of different devices: /device:TPU:1 before, /device:TPU:224 now
where the time goes in v1:
time: 37.8 us; the launch traced here: 37.7 us
  Pallas kernels  35.8 us (95%)
  local copies, waits for them, and re-layouts  1.88 us (5%)
    pallas_call x1, Pallas kernels, body(): pl.pallas_call(functools.partial(kernel, planes), out_shape=jax.ShapeDtyp...  35.8 us
    unnamed x1, local copies, waits for them, and re-layouts  1.88 us

profile of v1, /device:TPU:224, one launch (start us, length us, event | category | flops | bytes accessed | tf_op | source)
XLA Modules:
  0.0 37.7 jit_solution(13404982804936324752)
XLA Ops:
  0.0 35.8 %shard_map.82 = bf16[128,2048]{1,0:T(8,128)(2,1)} custom-call(bf16[128,2048]{1,0:T(8,128)(2,1)} %q_hbm.1, bf16[128,2048]{1,0:T(8,128)(2,1)} %k_hbm.1, bf16[128,2048]{1,0:T(8,128)(2,1)} %v_hbm.1, f32[3,3,2048]{2,1,0:T(4,128)} %taps_hbm.1, f32[16,2048]{1,0:T(8,128)} %bitcast.3, f32[16,2048]{1,0:T(8,128)} %bitcast.4, f32[16,128]{1,0:T(8,128)} %bitcast.5, ...), custom_call_target="tpu_custom_call" | custom-call | tf_op jit(solution)/shard_map/pallas_call | solution.py:339
  35.8 1.9 %copy.10 = bf16[128,2048]{1,0:T(8,128)(2,1)} copy(bf16[128,2048]{1,0:T(8,128)(2,1)} %shard_map.82) | data formatting | bytes 1048576

commit v2 on v0

v2 whole, which is shorter than its diff:
```python
import functools
import math

import jax
import jax.numpy as jnp
from jax import lax
from jax.experimental import pallas as pl
from jax.experimental.pallas import tpu as pltpu
from jax.sharding import PartitionSpec as P

MESH = pl.DeviceIdType.MESH
LANES = 128
ROWS = 8


def lanes(strip, count=1):
    return pl.ds(pl.multiple_of(strip * LANES, LANES), count * LANES)


def scratch(planes, toks, width, modes):
    f32, bf16 = jnp.float32, jnp.bfloat16
    strips, blocks = width // LANES, toks // ROWS
    wide = math.isqrt(strips)
    dma = pltpu.SemaphoreType.DMA
    return dict(
        q_in=pltpu.VMEM((toks, width), bf16),
        k_in=pltpu.VMEM((toks, width), bf16),
        v_in=pltpu.VMEM((toks, width), bf16),
        tails=pltpu.VMEM((ROWS, width), bf16),
        halos=pltpu.VMEM((ROWS, width), bf16),
        taps=pltpu.VMEM((3, 3, width), f32),
        rate=pltpu.VMEM((modes, width), f32),
        res=pltpu.VMEM((modes, width), f32),
        skip=pltpu.VMEM((strips, LANES), f32),
        w_in=pltpu.VMEM((width, width), bf16),
        qf=pltpu.VMEM((toks + ROWS, width), f32),
        kf=pltpu.VMEM((toks + ROWS, width), f32),
        vf=pltpu.VMEM((toks + ROWS, width), f32),
        x=pltpu.VMEM((toks, width), f32),
        y=pltpu.VMEM((toks, width), f32),
        gate=pltpu.VMEM((toks, width), f32),
        total=pltpu.VMEM((toks, width), f32),
        gated=pltpu.VMEM((2, toks, wide * LANES), bf16),
        gain=pltpu.VMEM((strips, modes, ROWS, LANES), f32),
        near=pltpu.VMEM((strips, ROWS, ROWS, LANES), f32),
        ahead=pltpu.VMEM((strips, LANES), f32),
        drop=pltpu.VMEM((strips, modes, LANES), f32),
        held=pltpu.VMEM((strips, blocks, modes, LANES), f32),
        edges=pltpu.VMEM((strips, ROWS, LANES), bf16),
        edges_in=pltpu.VMEM((strips, ROWS, LANES), bf16),
        rows_in=pltpu.VMEM((strips * ROWS, LANES), f32),
        heads=pltpu.VMEM((2, strips, LANES), f32),
        shift=pltpu.VMEM((strips, modes, LANES), f32),
        ends=pltpu.VMEM((strips, modes, LANES), f32),
        got=pltpu.VMEM((strips, modes, LANES), f32),
        sums=pltpu.VMEM((modes + ROWS, LANES), f32),
        carry=pltpu.VMEM((2, modes, LANES), f32),
        sums_in=pltpu.VMEM((planes, modes + ROWS, LANES), f32),
        starts=pltpu.VMEM((strips, modes, LANES), f32),
        starts_in=pltpu.VMEM((strips, modes, LANES), f32),
        load_sem=dma((15,)),
        halo_send=dma,
        halo_recv=dma,
        edge_send=dma((strips,)),
        edge_recv=dma((strips,)),
        up_send=dma((strips,)),
        up_recv=dma((strips,)),
        side_send=dma((planes,)),
        side_recv=dma((planes,)),
        down_send=dma((strips,)),
        down_recv=dma((strips,)),
        ready=pltpu.SemaphoreType.REGULAR((planes + 1,)),
    )


def kernel(planes, names, q_hbm, k_hbm, v_hbm, taps_hbm, rate_hbm, res_hbm, skip_hbm, w_hbm, out_ref, *refs):
    s = dict(zip(names, refs, strict=True))
    q_in, k_in, v_in, tails, halos, taps = (s[n] for n in ("q_in", "k_in", "v_in", "tails", "halos", "taps"))
    rate, res, skip, w_in, qf, kf, vf, x = (s[n] for n in ("rate", "res", "skip", "w_in", "qf", "kf", "vf", "x"))
    y, gate, total, gated, gain, near, ahead, drop = (
        s[n] for n in ("y", "gate", "total", "gated", "gain", "near", "ahead", "drop")
    )
    held, edges, edges_in, rows_in, heads = (s[n] for n in ("held", "edges", "edges_in", "rows_in", "heads"))
    shift, ends, got, sums, carry = (s[n] for n in ("shift", "ends", "got", "sums", "carry"))
    sums_in, starts, starts_in = (s[n] for n in ("sums_in", "starts", "starts_in"))

    f32, bf16 = jnp.float32, jnp.bfloat16
    toks, width = q_hbm.shape
    modes = rate_hbm.shape[0]
    strips, blocks = width // LANES, toks // ROWS
    members, wide = strips, math.isqrt(strips)
    chunk = wide * LANES
    half = strips // 2
    me = lax.axis_index("seq")
    plane, spot = me // members, me % members
    spot_y, spot_x = spot // wide, spot % wide
    first_plane = plane * members
    last = planes * members - 1

    def load(source, target, at):
        copy = pltpu.make_async_copy(source, target, s["load_sem"].at[at])
        copy.start()
        return copy

    rate_load = load(rate_hbm, rate, 3)
    taps_load = load(taps_hbm, taps, 4)
    k_loads, v_loads = [], []
    for c in range(2):
        cols = pl.ds(c * half * LANES, half * LANES)
        k_loads.append(load(k_hbm.at[:, cols], k_in.at[:, cols], 11 + 2 * c))
        v_loads.append(load(v_hbm.at[:, cols], v_in.at[:, cols], 12 + 2 * c))
    res_load = load(res_hbm, res, 5)
    skip_load = load(skip_hbm, skip, 6)
    q_load = load(q_hbm, q_in, 7)
    w_load = load(w_hbm, w_in, 8)

    barrier = pltpu.get_barrier_semaphore()

    def greet(device):
        pl.semaphore_signal(barrier, inc=1, device_id={"seq": device}, device_id_type=MESH)

    for i in range(members):

        @pl.when(spot != i)
        def _():
            greet(first_plane + i)

    for i in range(1, planes):

        @pl.when(plane < i)
        def _():
            greet(i * members + spot)

    after_end = (plane > 0) & (spot == 0)
    before_start = (plane < planes - 1) & (spot == members - 1)

    @pl.when(before_start)
    def _():
        greet(me + 1)

    def short(source, kind, start, count, cols):
        rows = [source[pl.ds(ROWS + start - lag, count), cols] for lag in range(3)]
        result = taps[kind, 0:1, cols] * rows[0] + taps[kind, 1:2, cols] * rows[1]
        return result + taps[kind, 2:3, cols] * rows[2]

    def mixed(start, count, cols):
        product = short(kf, 1, start, count, cols) * short(vf, 2, start, count, cols)
        x[pl.ds(start, count), cols] = product.astype(bf16).astype(f32)

    def first_pass(at):
        size = half * LANES
        cols = pl.ds(at * size, size)
        kf[0:ROWS, cols] = jnp.zeros((ROWS, size), f32)
        vf[0:ROWS, cols] = jnp.zeros((ROWS, size), f32)
        kf[pl.ds(ROWS, toks), cols] = k_in[:, cols].astype(f32)
        vf[pl.ds(ROWS, toks), cols] = v_in[:, cols].astype(f32)
        for block in range(blocks):
            mixed(block * ROWS, ROWS, cols)
        step = jnp.exp(-rate[:, cols])
        state = jnp.zeros((modes, size), f32)
        for t in range(2, toks):
            if t % ROWS == 0:
                for i in range(half):
                    held[at * half + i, t // ROWS] = state[:, i * LANES : (i + 1) * LANES]
            state = step * state + x[pl.ds(t, 1), cols]
        for i in range(half):
            ends[at * half + i] = state[:, i * LANES : (i + 1) * LANES]

    def remote(source, target, send, recv, device):
        return pltpu.make_async_remote_copy(
            src_ref=source, dst_ref=target, send_sem=send, recv_sem=recv,
            device_id={"seq": device}, device_id_type=MESH,
        )

    def edge(i):
        return remote(edges.at[i], edges_in.at[spot], s["edge_send"].at[i], s["edge_recv"].at[spot], first_plane + i)

    def up(i):
        return remote(ends.at[i], got.at[spot], s["up_send"].at[i], s["up_recv"].at[spot], first_plane + i)

    def side(i):
        return remote(sums, sums_in.at[plane], s["side_send"].at[i], s["side_recv"].at[plane], i * members + spot)

    def down(i):
        return remote(starts.at[i], starts_in.at[spot], s["down_send"].at[i], s["down_recv"].at[spot], first_plane + i)

    def halo(device):
        return remote(tails, halos, s["halo_send"], s["halo_recv"], device)

    rate_load.wait()
    taps_load.wait()
    k_loads[0].wait()
    v_loads[0].wait()
    first_pass(0)
    k_loads[1].wait()
    v_loads[1].wait()
    first_pass(1)
    for i in range(strips):
        cols = lanes(i)
        for j, ref in enumerate((k_in, v_in)):
            edges[i, 2 * j : 2 * j + 2] = ref[0:2, cols]
            edges[i, 4 + 2 * j : 6 + 2 * j] = ref[toks - 2 : toks, cols]
    pl.semaphore_wait(barrier, members - 1 + plane + jnp.where(after_end, 1, 0))
    def ring(d):
        return min(d, wide - d)

    hops = [(dy, dx) for dy in range(wide) for dx in range(wide) if dy + dx > 0]
    hops = sorted(hops, key=lambda d: -ring(d[0]) - ring(d[1]))
    peers = [lax.rem(spot_y + dy, wide) * wide + lax.rem(spot_x + dx, wide) for dy, dx in hops]
    for i in peers:
        edge(i).start()
        up(i).start()

    def hail(device, at):
        pl.semaphore_signal(s["ready"].at[at], inc=1, device_id={"seq": device}, device_id_type=MESH)

    for i in range(planes - 1):

        @pl.when(plane > i)
        def _():
            hail(i * members + spot, plane)

    @pl.when(after_end)
    def _():
        hail(me - 1, planes)

    got[spot] = ends[spot]
    edges_in[spot] = edges[spot]

    @pl.when(me == 0)
    def _():
        halos[...] = jnp.zeros((ROWS, width), bf16)

    for copy in (q_load, res_load, skip_load):
        copy.wait()

    for i, ref in enumerate((k_in, v_in, q_in)):
        tails[2 * i : 2 * i + 2] = ref[toks - 2 : toks]

    @pl.when(spot < members - 1)
    def _():
        halo(me + 1).start()

    places = lax.broadcasted_iota(jnp.int32, (ROWS, LANES), 0)
    later = (places + 1).astype(f32)

    def tabulate(strip, _):
        mine = lanes(strip)
        fade = rate[:, mine]
        scale = res[:, mine] * jnp.sqrt(1.0 - jnp.exp(-2.0 * fade))
        drop[strip] = jnp.exp(-float(ROWS) * fade)
        ahead[pl.ds(strip, 1), :] = jnp.sum(scale * jnp.exp(fade), axis=0, keepdims=True)
        after = jnp.zeros((ROWS, LANES), f32)
        for m in range(modes):
            table = jnp.exp(-later * rate[pl.ds(m, 1), mine]) * scale[m : m + 1]
            gain[strip, m] = table
            after = after + table
        now = jnp.sum(scale, axis=0, keepdims=True) + skip[pl.ds(strip, 1), :]
        taper = jnp.where(places == 0, now, pltpu.roll(after, 1, 0))
        near[strip, 0] = taper
        for j in range(1, ROWS):
            near[strip, j] = jnp.where(places >= j, pltpu.roll(taper, j, 0), 0.0)
        return 0

    lax.fori_loop(0, strips, tabulate, 0)
    def gates(strip, _):
        cols = lanes(strip)
        qf[pl.ds(ROWS, toks), cols] = q_in[:, cols].astype(f32)
        for block in range(1, blocks):
            gate[pl.ds(block * ROWS, ROWS), cols] = short(qf, 0, block * ROWS, ROWS, cols)
        return 0

    lax.fori_loop(0, strips, gates, 0)
    def local(strip, _):
        mine = lanes(strip)
        for block in range(blocks):
            parts = [near[strip, j] * x[pl.ds(block * ROWS + j, 1), mine] for j in range(0 if block else 2, ROWS)]
            if block > 0:
                parts += [gain[strip, m] * held[strip, block, pl.ds(m, 1), :] for m in range(modes)]
            y[pl.ds(block * ROWS, ROWS), mine] = functools.reduce(jnp.add, parts)
        return 0

    lax.fori_loop(0, strips, local, 0)
    for i in range(members):

        @pl.when(spot != i)
        def _():
            remote(edges_in.at[i], edges_in.at[i], s["edge_send"].at[i], s["edge_recv"].at[i], me).wait_recv()

    mine = lanes(spot)
    fade = rate[:, mine]
    for i in range(members):
        rows_in[i * ROWS : (i + 1) * ROWS] = edges_in[i].astype(f32)
    sums[modes : modes + 4] = rows_in[0:4]
    sums[modes + 4 : modes + 8] = rows_in[members * ROWS - 4 : members * ROWS]

    def two_inputs(head, tail):
        pairs = []
        for kind, offset in ((1, 0), (2, 2)):
            now, then, older, old = head(offset), head(offset + 1), tail(4 + offset), tail(5 + offset)
            t = [taps[kind, lag : lag + 1, mine] for lag in range(3)]
            pairs.append(((t[0] * now + t[1] * old) + t[2] * older, (t[0] * then + t[1] * now) + t[2] * old))
        (k_first, k_second), (v_first, v_second) = pairs
        return [(k * v).astype(bf16).astype(f32) for k, v in ((k_first, v_first), (k_second, v_second))]

    fall = [jnp.exp(-(toks - 1.0 - i) * fade) for i in range(2)]
    rise = [jnp.exp((1.0 + i) * fade) for i in range(2)]
    rest = members - 1
    inner = two_inputs(
        lambda r: rows_in[pl.ds(ROWS + r, rest, stride=ROWS), :], lambda r: rows_in[pl.ds(r, rest, stride=ROWS), :]
    )
    for i, rows in enumerate(inner):
        heads[i, 0:rest] = rows
    for i in range(rest):
        shift[i] = fall[0] * heads[0, i : i + 1] + fall[1] * heads[1, i : i + 1]
    for i in range(members):

        @pl.when(spot != i)
        def _():
            remote(got.at[i], got.at[i], s["up_send"].at[i], s["up_recv"].at[i], me).wait_recv()

    long_step = jnp.exp(-float(toks) * fade)
    running = jnp.zeros((modes, LANES), f32)
    for i in range(members):
        starts[i] = running
        running = long_step * running + got[i]
        if i > 0:
            running = running + shift[i - 1]
    sums[0:modes] = running

    for i in range(1, planes):

        @pl.when(plane < i)
        def _():
            pl.semaphore_wait(s["ready"].at[i], 1)
            side(i).start()

    @pl.when(before_start)
    def _():
        pl.semaphore_wait(s["ready"].at[planes], 1)
        halo(me + 1).start()

    sums_in[plane] = sums[...]
    for i in range(rest):
        starts[i + 1] = starts[i + 1] + (rise[0] * heads[0, i : i + 1] + rise[1] * heads[1, i : i + 1])
    carry[0] = jnp.zeros((modes, LANES), f32)
    rest_step = jnp.exp(-float(toks * rest) * fade)
    powers = [jnp.exp(-float(toks * i) * fade) for i in range(rest)]
    for i in range(planes):

        @pl.when(plane >= i)
        def _():
            if i < planes - 1:

                @pl.when(plane > i)
                def _():
                    remote(sums_in.at[i], sums_in.at[i], s["side_send"].at[i], s["side_recv"].at[i], me).wait_recv()

            def row(at, r):
                return sums_in[at, modes + r : modes + r + 1, :]

            none = jnp.zeros((1, LANES), f32)
            x_first, x_second = two_inputs(lambda r: row(i, r), lambda r: row(i - 1, r) if i else none)
            moved = long_step * carry[0] + (fall[0] * x_first + fall[1] * x_second)

            @pl.when(plane == i)
            def _():
                starts[0] = carry[0] + (rise[0] * x_first + rise[1] * x_second)
                carry[1] = moved

            @pl.when(plane > i)
            def _():
                carry[0] = rest_step * moved + sums_in[i, 0:modes]

    moved = carry[1]
    for i in range(rest):
        starts[i + 1] = starts[i + 1] + powers[i] * moved

    for i in peers:
        down(i).start()

    starts_in[spot] = starts[spot]
    @pl.when(me > 0)
    def _():
        halo(me - 1).wait_recv()

    def patch(strip, _):
        cols = lanes(strip)
        kf[ROWS - 2 : ROWS, cols] = halos[0:2, cols].astype(f32)
        vf[ROWS - 2 : ROWS, cols] = halos[2:4, cols].astype(f32)
        qf[ROWS - 2 : ROWS, cols] = halos[4:6, cols].astype(f32)
        product = (short(kf, 1, 0, ROWS, cols) * short(vf, 2, 0, ROWS, cols)).astype(bf16).astype(f32)
        direct = jnp.where(places < 2, skip[pl.ds(strip, 1), :] * product, 0.0)
        extra = jnp.where(places == 0, ahead[pl.ds(strip, 1), :] * product[1:2], 0.0)
        y[0:ROWS, cols] = y[0:ROWS, cols] + (direct - extra)
        gate[0:ROWS, cols] = short(qf, 0, 0, ROWS, cols)
        return 0

    lax.fori_loop(0, strips, patch, 0)
    column = min(256, width)

    def fetch(at):
        for i in range(wide):
            strip = at * wide + i

            @pl.when(spot != strip)
            def _():
                remote(
                    starts_in.at[strip], starts_in.at[strip], s["down_send"].at[strip], s["down_recv"].at[strip], me
                ).wait_recv()

    def finish(at, slot):
        for i in range(wide):
            strip = at * wide + i
            cols = lanes(strip)
            terms = [gain[strip, m] * starts_in[strip, pl.ds(m, 1), :] for m in range(modes)]
            fades = [jnp.broadcast_to(drop[strip, pl.ds(m, 1), :], (ROWS, LANES)) for m in range(modes)]
            for block in range(blocks):
                rows = pl.ds(block * ROWS, ROWS)
                result = y[rows, cols]
                for m in range(modes):
                    result = result + terms[m]
                if block < blocks - 1:
                    terms = [term * fade for term, fade in zip(terms, fades, strict=True)]
                x[rows, cols] = gate[rows, cols] * result.astype(bf16).astype(f32)
            gated[slot, :, i * LANES : (i + 1) * LANES] = x[:, cols].astype(bf16)

    def project(at, slot, begins, stops):
        rows = pl.ds(pl.multiple_of(at * chunk, chunk), chunk)
        for n in range(width // column):
            cols = slice(n * column, (n + 1) * column)
            part = jnp.dot(gated[slot], w_in[rows, cols], preferred_element_type=f32)
            if not begins:
                part = part + total[:, cols]
            if stops:
                out_ref[:, cols] = part.astype(out_ref.dtype)
            else:
                total[:, cols] = part

    order = sorted(range(wide), key=ring)
    turns = [lax.rem(spot_y + d, wide) for d in order]
    fetch(turns[0])
    finish(turns[0], 0)
    w_load.wait()
    for j in range(1, wide):
        fetch(turns[j])
        project(turns[j - 1], (j - 1) % 2, j == 1, False)
        finish(turns[j], j % 2)
    project(turns[wide - 1], (wide - 1) % 2, wide == 1, True)
    @pl.when(me < last)
    def _():
        halo(me + 1).wait_send()

    for i in peers:
        edge(i).wait_send()
        up(i).wait_send()
        down(i).wait_send()

    for i in range(1, planes):

        @pl.when(plane < i)
        def _():
            side(i).wait_send()


def body(planes, queries, keys, values, short_taps, decay, residue, skip, w_out):
    toks, width = queries.shape
    modes = decay.shape[1]
    held = scratch(planes, toks, width, modes)
    outside = pl.BlockSpec(memory_space=pltpu.HBM)
    return pl.pallas_call(
        functools.partial(kernel, planes, tuple(held)),
        out_shape=jax.ShapeDtypeStruct((toks, width), jnp.bfloat16),
        in_specs=[outside] * 8,
        out_specs=pl.BlockSpec(memory_space=pltpu.VMEM),
        scratch_shapes=list(held.values()),
        compiler_params=pltpu.CompilerParams(
            collective_id=0, has_side_effects=True, vmem_limit_bytes=48 * 1024 * 1024
        ),
    )(
        *(
            pltpu.with_memory_space_constraint(value, pltpu.HBM)
            for value in (
                queries, keys, values, short_taps, decay.T, residue.T,
                skip.reshape(width // LANES, LANES), w_out,
            )
        )
    )


def solution(mesh):
    split = P(("rep", "seq"), None)
    placed = (split, split, split, P(), P(), P(), P(), P())

    def run(queries, *rest):
        planes = mesh.shape["seq"] * LANES // queries.shape[1]
        return body(planes, queries, *rest)

    return jax.shard_map(run, mesh=mesh, in_specs=placed, out_specs=split, check_vma=False)
```

time: 92.5 us -> 22.8 us (0.25)
  the two profiles are of different devices: /device:TPU:1 before, /device:TPU:224 now
where the time goes in v2:
time: 22.8 us; the launch traced here: 22.7 us
  Pallas kernels  21.9 us (96%)
  local copies, waits for them, and re-layouts  0.8 us (4%)
    pallas_call x1, Pallas kernels, body(): pl.pallas_call(functools.partial(kernel, planes, tuple(held)), out_shape=...  21.9 us
    unnamed x1, local copies, waits for them, and re-layouts  0.8 us

profile of v2, /device:TPU:224, one launch (start us, length us, event | category | flops | bytes accessed | tf_op | source)
XLA Modules:
  0.0 22.7 jit_solution(9849760176658168313)
XLA Ops:
  0.0 21.9 %shard_map.82 = bf16[128,2048]{1,0:T(8,128)(2,1)S(1)} custom-call(bf16[128,2048]{1,0:T(8,128)(2,1)} %q_hbm.1, bf16[128,2048]{1,0:T(8,128)(2,1)} %k_hbm.1, bf16[128,2048]{1,0:T(8,128)(2,1)} %v_hbm.1, f32[3,3,2048]{2,1,0:T(4,128)} %taps_hbm.1, f32[16,2048]{1,0:T(8,128)} %bitcast.3, f32[16,2048]{1,0:T(8,128)} %bitcast.4, f32[16,128]{1,0:T(8,128)} %bitcast.5, ...), custom_call_target="tpu_custom_call" | custom-call | tf_op jit(solution)/shard_map/pallas_call | solution.py:471
  21.9 0.8 %copy.10 = bf16[128,2048]{1,0:T(8,128)(2,1)} copy(bf16[128,2048]{1,0:T(8,128)(2,1)S(1)} %shard_map.82) | data formatting | bytes 1048576

commit v3 on v2

--- a/solution.py
+++ b/solution.py
@@ -24,18 +24,15 @@
     dma = pltpu.SemaphoreType.DMA
     return dict(
         q_in=pltpu.VMEM((toks, width), bf16),
-        k_in=pltpu.VMEM((toks, width), bf16),
-        v_in=pltpu.VMEM((toks, width), bf16),
+        kv_in=pltpu.VMEM((2, toks, width), bf16),
         tails=pltpu.VMEM((ROWS, width), bf16),
         halos=pltpu.VMEM((ROWS, width), bf16),
         taps=pltpu.VMEM((3, 3, width), f32),
-        rate=pltpu.VMEM((modes, width), f32),
-        res=pltpu.VMEM((modes, width), f32),
+        modal=pltpu.VMEM((2, modes, width), f32),
         skip=pltpu.VMEM((strips, LANES), f32),
         w_in=pltpu.VMEM((width, width), bf16),
         qf=pltpu.VMEM((toks + ROWS, width), f32),
-        kf=pltpu.VMEM((toks + ROWS, width), f32),
-        vf=pltpu.VMEM((toks + ROWS, width), f32),
+        kv=pltpu.VMEM((strips, 2 * (toks + ROWS), LANES), f32),
         x=pltpu.VMEM((toks, width), f32),
         y=pltpu.VMEM((toks, width), f32),
         gate=pltpu.VMEM((toks, width), f32),
@@ -58,25 +55,27 @@
         sums_in=pltpu.VMEM((planes, modes + ROWS, LANES), f32),
         starts=pltpu.VMEM((strips, modes, LANES), f32),
         starts_in=pltpu.VMEM((strips, modes, LANES), f32),
-        load_sem=dma((15,)),
+        load_sem=dma((7,)),
         halo_send=dma,
         halo_recv=dma,
-        edge_send=dma((strips,)),
-        edge_recv=dma((strips,)),
-        up_send=dma((strips,)),
-        up_recv=dma((strips,)),
-        side_send=dma((planes,)),
-        side_recv=dma((planes,)),
-        down_send=dma((strips,)),
-        down_recv=dma((strips,)),
-        ready=pltpu.SemaphoreType.REGULAR((planes + 1,)),
+        edge_send=dma,
+        edge_recv=dma,
+        up_send=dma,
+        up_recv=dma,
+        side_send=dma((planes - 1,)),
+        side_recv=dma((planes - 1,)),
+        down_send=dma,
+        down_recv=dma((wide + 1,)),
+        ready=pltpu.SemaphoreType.REGULAR((planes,)),
     )
 
 
 def kernel(planes, names, q_hbm, k_hbm, v_hbm, taps_hbm, rate_hbm, res_hbm, skip_hbm, w_hbm, out_ref, *refs):
     s = dict(zip(names, refs, strict=True))
-    q_in, k_in, v_in, tails, halos, taps = (s[n] for n in ("q_in", "k_in", "v_in", "tails", "halos", "taps"))
-    rate, res, skip, w_in, qf, kf, vf, x = (s[n] for n in ("rate", "res", "skip", "w_in", "qf", "kf", "vf", "x"))
+    q_in, kv_in, tails, halos, modal = (s[n] for n in ("q_in", "kv_in", "tails", "halos", "modal"))
+    taps, skip, w_in, qf, kv, x = (s[n] for n in ("taps", "skip", "w_in", "qf", "kv", "x"))
+    k_in, v_in = kv_in.at[0], kv_in.at[1]
+    rate, res = modal.at[0], modal.at[1]
     y, gate, total, gated, gain, near, ahead, drop = (
         s[n] for n in ("y", "gate", "total", "gated", "gain", "near", "ahead", "drop")
     )
@@ -89,7 +88,6 @@
     modes = rate_hbm.shape[0]
     strips, blocks = width // LANES, toks // ROWS
     members, wide = strips, math.isqrt(strips)
-    chunk = wide * LANES
     half = strips // 2
     me = lax.axis_index("seq")
     plane, spot = me // members, me % members
@@ -102,28 +100,27 @@
         copy.start()
         return copy
 
-    rate_load = load(rate_hbm, rate, 3)
-    taps_load = load(taps_hbm, taps, 4)
-    k_loads, v_loads = [], []
-    for c in range(2):
-        cols = pl.ds(c * half * LANES, half * LANES)
-        k_loads.append(load(k_hbm.at[:, cols], k_in.at[:, cols], 11 + 2 * c))
-        v_loads.append(load(v_hbm.at[:, cols], v_in.at[:, cols], 12 + 2 * c))
-    res_load = load(res_hbm, res, 5)
-    skip_load = load(skip_hbm, skip, 6)
-    q_load = load(q_hbm, q_in, 7)
-    w_load = load(w_hbm, w_in, 8)
+    load(rate_hbm, rate, 0)
+    load(res_hbm, res, 0)
+    taps_load = load(taps_hbm, taps, 1)
+    halves = [pl.ds(c * half * LANES, half * LANES) for c in range(2)]
+    for c, cols in enumerate(halves):
+        load(k_hbm.at[:, cols], k_in.at[:, cols], 2 + c)
+        load(v_hbm.at[:, cols], v_in.at[:, cols], 2 + c)
 
     barrier = pltpu.get_barrier_semaphore()
 
     def greet(device):
         pl.semaphore_signal(barrier, inc=1, device_id={"seq": device}, device_id_type=MESH)
 
-    for i in range(members):
-
-        @pl.when(spot != i)
-        def _():
-            greet(first_plane + i)
+    def ring(d):
+        return min(d, wide - d)
+
+    hops = [(dy, dx) for dy in range(wide) for dx in range(wide) if dy + dx > 0]
+    hops = sorted(hops, key=lambda d: -ring(d[0]) - ring(d[1]))
+    peers = [lax.rem(spot_y + dy, wide) * wide + lax.rem(spot_x + dx, wide) for dy, dx in hops]
+    for i in peers:
+        greet(first_plane + i)
 
     for i in range(1, planes):
 
@@ -131,40 +128,59 @@
         def _():
             greet(i * members + spot)
 
-    after_end = (plane > 0) & (spot == 0)
-    before_start = (plane < planes - 1) & (spot == members - 1)
-
-    @pl.when(before_start)
+    closing = (spot == members - 1) & (plane < planes - 1)
+    opening = (spot == 0) & (plane > 0)
+
+    @pl.when(closing)
     def _():
         greet(me + 1)
+
+    skip_load = load(skip_hbm, skip, 4)
+    q_load = load(q_hbm, q_in, 5)
+    w_load = load(w_hbm, w_in, 6)
+
+    def arrive(ref, sem):
+        pltpu.make_async_copy(ref, ref, sem).wait()
 
     def short(source, kind, start, count, cols):
         rows = [source[pl.ds(ROWS + start - lag, count), cols] for lag in range(3)]
         result = taps[kind, 0:1, cols] * rows[0] + taps[kind, 1:2, cols] * rows[1]
         return result + taps[kind, 2:3, cols] * rows[2]
 
-    def mixed(start, count, cols):
-        product = short(kf, 1, start, count, cols) * short(vf, 2, start, count, cols)
-        x[pl.ds(start, count), cols] = product.astype(bf16).astype(f32)
+    def paired(strip, kind, start):
+        return kv[strip, pl.ds(2 * (ROWS + start) + kind - 1, ROWS, stride=2), :]
+
+    def mixed(strip, start, weights):
+        parts = []
+        for kind in (1, 2):
+            rows = [paired(strip, kind, start - lag) for lag in range(3)]
+            t = weights[kind]
+            parts.append((t[0] * rows[0] + t[1] * rows[1]) + t[2] * rows[2])
+        return (parts[0] * parts[1]).astype(bf16).astype(f32)
+
+    def taps_of(cols):
+        return [None] + [[taps[kind, lag : lag + 1, cols] for lag in range(3)] for kind in (1, 2)]
 
     def first_pass(at):
-        size = half * LANES
-        cols = pl.ds(at * size, size)
-        kf[0:ROWS, cols] = jnp.zeros((ROWS, size), f32)
-        vf[0:ROWS, cols] = jnp.zeros((ROWS, size), f32)
-        kf[pl.ds(ROWS, toks), cols] = k_in[:, cols].astype(f32)
-        vf[pl.ds(ROWS, toks), cols] = v_in[:, cols].astype(f32)
-        for block in range(blocks):
-            mixed(block * ROWS, ROWS, cols)
-        step = jnp.exp(-rate[:, cols])
-        state = jnp.zeros((modes, size), f32)
+        strips_now = range(at * half, (at + 1) * half)
+        for strip in strips_now:
+            cols = pl.ds(strip * LANES, LANES)
+            weights = taps_of(cols)
+            kv[strip, 0 : 2 * ROWS] = jnp.zeros((2 * ROWS, LANES), f32)
+            for kind, ref in ((1, k_in), (2, v_in)):
+                kv[strip, pl.ds(2 * ROWS + kind - 1, toks, stride=2), :] = ref[:, cols].astype(f32)
+            for block in range(blocks):
+                x[pl.ds(block * ROWS, ROWS), cols] = mixed(strip, block * ROWS, weights)
+        steps = [jnp.exp(-rate[:, pl.ds(strip * LANES, LANES)]) for strip in strips_now]
+        states = [jnp.zeros((modes, LANES), f32) for _ in strips_now]
         for t in range(2, toks):
             if t % ROWS == 0:
-                for i in range(half):
-                    held[at * half + i, t // ROWS] = state[:, i * LANES : (i + 1) * LANES]
-            state = step * state + x[pl.ds(t, 1), cols]
-        for i in range(half):
-            ends[at * half + i] = state[:, i * LANES : (i + 1) * LANES]
+                for strip, state in zip(strips_now, states, strict=True):
+                    held[strip, t // ROWS] = state
+            rows = [x[pl.ds(t, 1), pl.ds(strip * LANES, LANES)] for strip in strips_now]
+            states = [step * state + row for step, state, row in zip(steps, states, rows, strict=True)]
+        for strip, state in zip(strips_now, states, strict=True):
+            ends[strip] = state
 
     def remote(source, target, send, recv, device):
         return pltpu.make_async_remote_copy(
@@ -173,40 +189,34 @@
         )
 
     def edge(i):
-        return remote(edges.at[i], edges_in.at[spot], s["edge_send"].at[i], s["edge_recv"].at[spot], first_plane + i)
+        return remote(edges.at[i], edges_in.at[spot], s["edge_send"], s["edge_recv"], first_plane + i)
 
     def up(i):
-        return remote(ends.at[i], got.at[spot], s["up_send"].at[i], s["up_recv"].at[spot], first_plane + i)
+        return remote(ends.at[i], got.at[spot], s["up_send"], s["up_recv"], first_plane + i)
 
     def side(i):
-        return remote(sums, sums_in.at[plane], s["side_send"].at[i], s["side_recv"].at[plane], i * members + spot)
-
-    def down(i):
-        return remote(starts.at[i], starts_in.at[spot], s["down_send"].at[i], s["down_recv"].at[spot], first_plane + i)
+        return remote(
+            sums, sums_in.at[plane], s["side_send"].at[i - 1], s["side_recv"].at[plane], i * members + spot
+        )
+
+    def down(i, group):
+        return remote(starts.at[i], starts_in.at[spot], s["down_send"], s["down_recv"].at[group], first_plane + i)
 
     def halo(device):
         return remote(tails, halos, s["halo_send"], s["halo_recv"], device)
 
-    rate_load.wait()
+    arrive(modal, s["load_sem"].at[0])
     taps_load.wait()
-    k_loads[0].wait()
-    v_loads[0].wait()
+    arrive(kv_in.at[:, :, halves[0]], s["load_sem"].at[2])
     first_pass(0)
-    k_loads[1].wait()
-    v_loads[1].wait()
+    arrive(kv_in.at[:, :, halves[1]], s["load_sem"].at[3])
     first_pass(1)
     for i in range(strips):
         cols = lanes(i)
         for j, ref in enumerate((k_in, v_in)):
             edges[i, 2 * j : 2 * j + 2] = ref[0:2, cols]
             edges[i, 4 + 2 * j : 6 + 2 * j] = ref[toks - 2 : toks, cols]
-    pl.semaphore_wait(barrier, members - 1 + plane + jnp.where(after_end, 1, 0))
-    def ring(d):
-        return min(d, wide - d)
-
-    hops = [(dy, dx) for dy in range(wide) for dx in range(wide) if dy + dx > 0]
-    hops = sorted(hops, key=lambda d: -ring(d[0]) - ring(d[1]))
-    peers = [lax.rem(spot_y + dy, wide) * wide + lax.rem(spot_x + dx, wide) for dy, dx in hops]
+    pl.semaphore_wait(barrier, members - 1 + plane + jnp.where(opening, 1, 0))
     for i in peers:
         edge(i).start()
         up(i).start()
@@ -218,11 +228,11 @@
 
         @pl.when(plane > i)
         def _():
-            hail(i * members + spot, plane)
-
-    @pl.when(after_end)
-    def _():
-        hail(me - 1, planes)
+            hail(i * members + spot, plane - 1)
+
+    @pl.when(opening)
+    def _():
+        hail(me - 1, planes - 1)
 
     got[spot] = ends[spot]
     edges_in[spot] = edges[spot]
@@ -231,8 +241,8 @@
     def _():
         halos[...] = jnp.zeros((ROWS, width), bf16)
 
-    for copy in (q_load, res_load, skip_load):
-        copy.wait()
+    q_load.wait()
+    skip_load.wait()
 
     for i, ref in enumerate((k_in, v_in, q_in)):
         tails[2 * i : 2 * i + 2] = ref[toks - 2 : toks]
@@ -280,13 +290,10 @@
             y[pl.ds(block * ROWS, ROWS), mine] = functools.reduce(jnp.add, parts)
         return 0
 
-    lax.fori_loop(0, strips, local, 0)
-    for i in range(members):
-
-        @pl.when(spot != i)
-        def _():
-            remote(edges_in.at[i], edges_in.at[i], s["edge_send"].at[i], s["edge_recv"].at[i], me).wait_recv()
-
+    early = strips * 3 // 4
+    lax.fori_loop(0, early, local, 0)
+    others = pl.ds(0, members - 1)
+    arrive(edges_in.at[others], s["edge_recv"])
     mine = lanes(spot)
     fade = rate[:, mine]
     for i in range(members):
@@ -313,12 +320,7 @@
         heads[i, 0:rest] = rows
     for i in range(rest):
         shift[i] = fall[0] * heads[0, i : i + 1] + fall[1] * heads[1, i : i + 1]
-    for i in range(members):
-
-        @pl.when(spot != i)
-        def _():
-            remote(got.at[i], got.at[i], s["up_send"].at[i], s["up_recv"].at[i], me).wait_recv()
-
+    arrive(got.at[others], s["up_recv"])
     long_step = jnp.exp(-float(toks) * fade)
     running = jnp.zeros((modes, LANES), f32)
     for i in range(members):
@@ -328,16 +330,20 @@
             running = running + shift[i - 1]
     sums[0:modes] = running
 
+    def send_side(i):
+        pl.semaphore_wait(s["ready"].at[i - 1], 1)
+        side(i).start()
+
     for i in range(1, planes):
 
-        @pl.when(plane < i)
+        @pl.when(((plane > 0) & (plane < i)) | (plane == i - 1))
         def _():
-            pl.semaphore_wait(s["ready"].at[i], 1)
-            side(i).start()
-
-    @pl.when(before_start)
-    def _():
-        pl.semaphore_wait(s["ready"].at[planes], 1)
+            send_side(i)
+
+    lax.fori_loop(early, strips, local, 0)
+    @pl.when(closing)
+    def _():
+        pl.semaphore_wait(s["ready"].at[planes - 1], 1)
         halo(me + 1).start()
 
     sums_in[plane] = sums[...]
@@ -354,7 +360,7 @@
 
                 @pl.when(plane > i)
                 def _():
-                    remote(sums_in.at[i], sums_in.at[i], s["side_send"].at[i], s["side_recv"].at[i], me).wait_recv()
+                    arrive(sums_in.at[i], s["side_recv"].at[i])
 
             def row(at, r):
                 return sums_in[at, modes + r : modes + r + 1, :]
@@ -376,20 +382,33 @@
     for i in range(rest):
         starts[i + 1] = starts[i + 1] + powers[i] * moved
 
-    for i in peers:
-        down(i).start()
+    reach = sorted(range(wide), key=ring)
+    pair = 2
+    for i, (dy, dx) in zip(peers, hops, strict=True):
+        group = reach.index((wide - dy) % wide)
+        if group == wide - 1:
+            across = lax.rem(spot_x // pair - lax.rem(spot_x + dx, wide) // pair + wide, wide // pair)
+            group = group + across
+        down(i, group).start()
+
+    @pl.when(plane == 0)
+    def _():
+        for i in range(2, planes):
+            send_side(i)
 
     starts_in[spot] = starts[spot]
     @pl.when(me > 0)
     def _():
-        halo(me - 1).wait_recv()
+        arrive(halos, s["halo_recv"])
 
     def patch(strip, _):
         cols = lanes(strip)
-        kf[ROWS - 2 : ROWS, cols] = halos[0:2, cols].astype(f32)
-        vf[ROWS - 2 : ROWS, cols] = halos[2:4, cols].astype(f32)
+        for kind in (1, 2):
+            kv[strip, pl.ds(2 * (ROWS - 2) + kind - 1, 2, stride=2), :] = halos[
+                2 * kind - 2 : 2 * kind, cols
+            ].astype(f32)
         qf[ROWS - 2 : ROWS, cols] = halos[4:6, cols].astype(f32)
-        product = (short(kf, 1, 0, ROWS, cols) * short(vf, 2, 0, ROWS, cols)).astype(bf16).astype(f32)
+        product = mixed(strip, 0, taps_of(cols))
         direct = jnp.where(places < 2, skip[pl.ds(strip, 1), :] * product, 0.0)
         extra = jnp.where(places == 0, ahead[pl.ds(strip, 1), :] * product[1:2], 0.0)
         y[0:ROWS, cols] = y[0:ROWS, cols] + (direct - extra)
@@ -399,37 +418,33 @@
     lax.fori_loop(0, strips, patch, 0)
     column = min(256, width)
 
-    def fetch(at):
-        for i in range(wide):
-            strip = at * wide + i
-
-            @pl.when(spot != strip)
-            def _():
-                remote(
-                    starts_in.at[strip], starts_in.at[strip], s["down_send"].at[strip], s["down_recv"].at[strip], me
-                ).wait_recv()
-
-    def finish(at, slot):
-        for i in range(wide):
-            strip = at * wide + i
+    def fetch(j):
+        count = len(turns[j]) - (j == 0)
+        arrive(starts_in.at[pl.ds(0, count)], s["down_recv"].at[j])
+
+    def finish(strips_now, slot):
+        for i, strip in enumerate(strips_now):
             cols = lanes(strip)
             terms = [gain[strip, m] * starts_in[strip, pl.ds(m, 1), :] for m in range(modes)]
             fades = [jnp.broadcast_to(drop[strip, pl.ds(m, 1), :], (ROWS, LANES)) for m in range(modes)]
-            for block in range(blocks):
-                rows = pl.ds(block * ROWS, ROWS)
-                result = y[rows, cols]
-                for m in range(modes):
-                    result = result + terms[m]
-                if block < blocks - 1:
-                    terms = [term * fade for term, fade in zip(terms, fades, strict=True)]
-                x[rows, cols] = gate[rows, cols] * result.astype(bf16).astype(f32)
-            gated[slot, :, i * LANES : (i + 1) * LANES] = x[:, cols].astype(bf16)
-
-    def project(at, slot, begins, stops):
-        rows = pl.ds(pl.multiple_of(at * chunk, chunk), chunk)
+            for block in range(0, blocks, 2):
+                results = []
+                for b in (block, block + 1):
+                    result = y[pl.ds(b * ROWS, ROWS), cols]
+                    for m in range(modes):
+                        result = result + terms[m]
+                    if b < blocks - 1:
+                        terms = [term * fade for term, fade in zip(terms, fades, strict=True)]
+                    results.append(gate[pl.ds(b * ROWS, ROWS), cols] * result.astype(bf16).astype(f32))
+                both = jnp.concatenate(results, axis=0).astype(bf16)
+                gated[slot, block * ROWS : (block + 2) * ROWS, i * LANES : (i + 1) * LANES] = both
+
+    def project(strips_now, slot, begins, stops):
+        size = len(strips_now) * LANES
+        rows = pl.ds(pl.multiple_of(strips_now[0] * LANES, size), size)
         for n in range(width // column):
             cols = slice(n * column, (n + 1) * column)
-            part = jnp.dot(gated[slot], w_in[rows, cols], preferred_element_type=f32)
+            part = jnp.dot(gated[slot, :, 0:size], w_in[rows, cols], preferred_element_type=f32)
             if not begins:
                 part = part + total[:, cols]
             if stops:
@@ -437,30 +452,37 @@
             else:
                 total[:, cols] = part
 
-    order = sorted(range(wide), key=ring)
-    turns = [lax.rem(spot_y + d, wide) for d in order]
-    fetch(turns[0])
+    turns = []
+    for dy in reach:
+        first = lax.rem(spot_y + dy, wide) * wide
+        if dy == reach[-1]:
+            for dx in range(0, wide, pair):
+                at = first + lax.rem(spot_x // pair * pair + dx, wide)
+                turns.append([at + i for i in range(pair)])
+        else:
+            turns.append([first + i for i in range(wide)])
+    count = len(turns)
+    fetch(0)
     finish(turns[0], 0)
     w_load.wait()
-    for j in range(1, wide):
-        fetch(turns[j])
+    for j in range(1, count):
+        fetch(j)
         project(turns[j - 1], (j - 1) % 2, j == 1, False)
         finish(turns[j], j % 2)
-    project(turns[wide - 1], (wide - 1) % 2, wide == 1, True)
-    @pl.when(me < last)
-    def _():
-        halo(me + 1).wait_send()
-
-    for i in peers:
-        edge(i).wait_send()
-        up(i).wait_send()
-        down(i).wait_send()
+    project(turns[count - 1], (count - 1) % 2, count == 1, True)
+    @pl.when((spot < members - 1) | closing)
+    def _():
+        arrive(tails, s["halo_send"])
+
+    arrive(edges.at[others], s["edge_send"])
+    arrive(ends.at[others], s["up_send"])
+    arrive(starts.at[others], s["down_send"])
 
     for i in range(1, planes):
 
         @pl.when(plane < i)
         def _():
-            side(i).wait_send()
+            arrive(sums, s["side_send"].at[i - 1])
 
 
 def body(planes, queries, keys, values, short_taps, decay, residue, skip, w_out):

time: 22.8 us -> 21.6 us (0.947)
  Pallas kernels: 21.9 us -> 20.7 us
    pallas_call x1, Pallas kernels: 21.9 us -> 20.7 us  [body(): pl.pallas_call(functools.partial(kernel, planes, tuple(held)), out_shape=...]
where the time goes in v3:
time: 21.6 us; the launch traced here: 21.5 us
  Pallas kernels  20.7 us (96%)
  local copies, waits for them, and re-layouts  0.8 us (4%)
    pallas_call x1, Pallas kernels, body(): pl.pallas_call(functools.partial(kernel, planes, tuple(held)), out_shape=...  20.7 us
    unnamed x1, local copies, waits for them, and re-layouts  0.8 us

profile of v3, /device:TPU:224, one launch (start us, length us, event | category | flops | bytes accessed | tf_op | source)
XLA Modules:
  0.0 21.5 jit_solution(523757447250542756)
XLA Ops:
  0.0 20.7 %shard_map.82 = bf16[128,2048]{1,0:T(8,128)(2,1)S(1)} custom-call(bf16[128,2048]{1,0:T(8,128)(2,1)} %q_hbm.1, bf16[128,2048]{1,0:T(8,128)(2,1)} %k_hbm.1, bf16[128,2048]{1,0:T(8,128)(2,1)} %v_hbm.1, f32[3,3,2048]{2,1,0:T(4,128)} %taps_hbm.1, f32[16,2048]{1,0:T(8,128)} %bitcast.3, f32[16,2048]{1,0:T(8,128)} %bitcast.4, f32[16,128]{1,0:T(8,128)} %bitcast.5, ...), custom_call_target="tpu_custom_call" | custom-call | tf_op jit(solution)/shard_map/pallas_call | solution.py:493
  20.7 0.8 %copy.10 = bf16[128,2048]{1,0:T(8,128)(2,1)} copy(bf16[128,2048]{1,0:T(8,128)(2,1)S(1)} %shard_map.82) | data formatting | bytes 1048576
